TPU v7x, 32 devices: a whole 2x2x4 slice. The times are simulated.
32 devices in a mesh: ctx: 16 (over z, y, x), head: 2 (over core).
Axes of the slice: x: 2, y: 2, z: 4, core: 2. Of those that a mesh axis runs over, the one named last changes fastest.
Arguments:
- queries: bfloat16 [4096, 4096], P('ctx', 'head'), may hold values from -200 to 200
- span_keys: bfloat16 [4096, 4096], P('ctx', 'head'), may hold values from -6 to 6
- span_values: bfloat16 [4096, 4096], P('ctx', 'head'), may hold values from -96 to 96
- cache_keys: bfloat16 [16384, 4096], P('ctx', 'head'), may hold values from -6 to 6
- cache_values: bfloat16 [16384, 4096], P('ctx', 'head'), may hold values from -96 to 96
- land_keys: bfloat16 [256, 4096], P('ctx', 'head'), may hold values from -4.5 to 4.5
- land_values: bfloat16 [256, 4096], P('ctx', 'head'), may hold values from -96 to 96
- out_weight: bfloat16 [4096, 4096], P('head', 'ctx'), may hold values from -0.09375 to 0.09375
- selection: int32 [64, 32, 4], P('ctx', 'head'), may hold values from 0 to 255, as said below
Outputs:
- projected: bfloat16 [4096, 4096], P('ctx', 'head')
Inputs may be any that keep to these rules, and one draw needn't show every extreme that they name: `selection`: the 4 blocks of one query group and head are distinct. Count block b as owned by ctx index b // 16. Over all groups and heads of one device (one index of ctx and one of head), the selections within one owner's blocks number at most 32 and form at most 8 distinct pairs of block and head; some owner receives exactly that many of both from every device.
All inputs are finite; a program needn't handle non-finite values.
Results may differ from a plain program's by a relative error of at most 0.015.
Values may be sent and summed in bfloat16 or wider, within the bound.
No kernel may reach another device: no remote copies, remote signals or barrier semaphores. Data moves between devices by JAX's collectives and lax.ppermute only.
A program may use at most 128 MiB of HBM per device.

v0:
```python
import math
import jax
import jax.numpy as jnp
from jax import lax
from jax.sharding import PartitionSpec as P

BLOCK = 64


def local(
    queries,
    span_keys,
    span_values,
    cache_keys,
    cache_values,
    land_keys,
    land_values,
    out_weight,
    selection,
):
    query_rows, row_width = queries.shape
    groups, head_dev, pick_count = selection.shape
    head_size = row_width // head_dev
    blocks_dev = cache_keys.shape[0] // BLOCK
    devices = lax.axis_size("ctx")
    scaling = 1.0 / math.sqrt(head_size)
    query_heads = queries.reshape(query_rows, head_dev, head_size)
    run_max = jnp.full((head_dev, query_rows), -jnp.inf, jnp.float32)
    run_sum = jnp.zeros((head_dev, query_rows), jnp.float32)
    run_acc = jnp.zeros((head_dev, query_rows, head_size), jnp.float32)
    key_piece = lax.all_gather(land_keys, "ctx", axis=0, tiled=True).reshape(
        -1, head_dev, head_size
    )
    value_piece = lax.all_gather(land_values, "ctx", axis=0, tiled=True).reshape(
        -1, head_dev, head_size
    )
    scores = (
        jnp.einsum("qhd,nhd->hqn", query_heads, key_piece, preferred_element_type=jnp.float32)
        * scaling
    )
    new_max = jnp.max(scores, axis=2)
    weights = jnp.exp(scores - new_max[:, :, None])
    factor = jnp.exp(run_max - new_max)
    new_sum = run_sum * factor + jnp.sum(weights, axis=2)
    new_acc = run_acc * factor[:, :, None] + jnp.einsum(
        "hqn,nhd->hqd",
        weights.astype(jnp.bfloat16),
        value_piece,
        preferred_element_type=jnp.float32,
    )
    request_count = groups * head_dev * pick_count
    owners_flat = (selection // blocks_dev).reshape(request_count)
    block_flat = (selection % blocks_dev).reshape(request_count)
    head_flat = jnp.broadcast_to(
        jnp.arange(head_dev, dtype=jnp.int32)[None, :, None], selection.shape
    ).reshape(request_count)
    request_order = jnp.arange(request_count)
    earlier = request_order[None, :] < request_order[:, None]
    same_owner = owners_flat[:, None] == owners_flat[None, :]
    distinct_most = (head_dev * 2 * pick_count + devices - 1) // devices
    key_blocks = cache_keys.reshape(blocks_dev, BLOCK, head_dev, head_size)
    value_blocks = cache_values.reshape(blocks_dev, BLOCK, head_dev, head_size)
    asked_pairs = jnp.stack([block_flat, head_flat], axis=1)
    pair_ids = selection.reshape(request_count) * head_dev + head_flat
    same_pair = pair_ids[:, None] == pair_ids[None, :]
    is_first = jnp.logical_not(jnp.any(same_pair & earlier, axis=1))
    first_rank = jnp.sum(same_owner & earlier & is_first[None, :], axis=1)
    slot_ids = jnp.sum(jnp.where(same_pair & is_first[None, :], first_rank[None, :], 0), axis=1)
    wanted = (
        jnp.zeros((devices, distinct_most, 2), jnp.int32).at[owners_flat, slot_ids].set(asked_pairs)
    )
    asked_for = lax.all_to_all(wanted, "ctx", split_axis=0, concat_axis=0, tiled=True)
    sent_keys = key_blocks[asked_for[:, :, 0], :, asked_for[:, :, 1], :]
    sent_values = value_blocks[asked_for[:, :, 0], :, asked_for[:, :, 1], :]
    fetched_keys = lax.all_to_all(sent_keys, "ctx", split_axis=0, concat_axis=0, tiled=True)
    fetched_values = lax.all_to_all(sent_values, "ctx", split_axis=0, concat_axis=0, tiled=True)
    owner_grid = owners_flat.reshape(selection.shape)
    slot_grid = slot_ids.reshape(selection.shape)
    chosen_keys = fetched_keys[owner_grid, slot_grid]
    chosen_values = fetched_values[owner_grid, slot_grid].reshape(
        groups, head_dev, pick_count * BLOCK, head_size
    )
    query_groups = query_heads.reshape(groups, BLOCK, head_dev, head_size)
    chosen_scores = (
        jnp.einsum(
            "gqhd,ghpkd->ghqpk", query_groups, chosen_keys, preferred_element_type=jnp.float32
        )
        * scaling
    )
    chosen_scores = chosen_scores.reshape(groups, head_dev, BLOCK, pick_count * BLOCK)
    local_keys = span_keys.reshape(groups, BLOCK, head_dev, head_size)
    local_values = span_values.reshape(groups, BLOCK, head_dev, head_size)
    causal = jnp.arange(BLOCK)[:, None] >= jnp.arange(BLOCK)[None, :]
    local_scores = (
        jnp.einsum("gqhd,gkhd->ghqk", query_groups, local_keys, preferred_element_type=jnp.float32)
        * scaling
    )
    local_scores = jnp.where(causal[None, None], local_scores, -jnp.inf)
    land_top = jnp.transpose(new_max.reshape(head_dev, groups, BLOCK), (1, 0, 2))
    land_total = jnp.transpose(new_sum.reshape(head_dev, groups, BLOCK), (1, 0, 2))
    land_part = jnp.transpose(new_acc.reshape(head_dev, groups, BLOCK, head_size), (1, 0, 2, 3))
    overall_top = jnp.maximum(
        jnp.maximum(land_top, jnp.max(chosen_scores, axis=3)), jnp.max(local_scores, axis=3)
    )
    land_weight = jnp.exp(land_top - overall_top)
    chosen_weights = jnp.exp(chosen_scores - overall_top[..., None])
    local_weights = jnp.exp(local_scores - overall_top[..., None])
    denominator = (
        land_total * land_weight + jnp.sum(chosen_weights, axis=3) + jnp.sum(local_weights, axis=3)
    )
    numerator = land_part * land_weight[..., None]
    numerator = numerator + jnp.einsum(
        "ghqn,ghnd->ghqd",
        chosen_weights.astype(jnp.bfloat16),
        chosen_values,
        preferred_element_type=jnp.float32,
    )
    numerator = numerator + jnp.einsum(
        "ghqk,gkhd->ghqd",
        local_weights.astype(jnp.bfloat16),
        local_values,
        preferred_element_type=jnp.float32,
    )
    attended = (numerator / denominator[..., None]).astype(jnp.bfloat16)
    attended = jnp.transpose(attended, (0, 2, 1, 3)).reshape(query_rows, row_width)
    partial_out = jnp.dot(
        attended,
        lax.all_gather(out_weight, "ctx", axis=1, tiled=True),
        preferred_element_type=jnp.float32,
    )
    summed = lax.psum_scatter(
        partial_out.astype(jnp.bfloat16), "head", scatter_dimension=1, tiled=True
    )
    return summed


def solution(mesh):
    placed = (
        P("ctx", "head"),
        P("ctx", "head"),
        P("ctx", "head"),
        P("ctx", "head"),
        P("ctx", "head"),
        P("ctx", "head"),
        P("ctx", "head"),
        P("head", "ctx"),
        P("ctx", "head", None),
    )
    return jax.shard_map(
        local, mesh=mesh, in_specs=placed, out_specs=P("ctx", "head"), check_vma=False
    )
```

profile of v0, /device:TPU:0, one launch (start us, length us, event | category | flops | bytes accessed | tf_op | source)
XLA Modules:
  0.0 416.4 jit_solution(2511548139788343026)
XLA Ops:
  8.7 0.8 copy.133
  10.9 11.6 %scatter_fusion = s32[16,8,2]{2,1,0:T(8,128)S(1)} fusion(s32[16,8,2]{2,1,0:T(8,128)S(1)} %broadcast_in_dim.38, s32[256]{0:T(256)S(1)} %bitcast.109, s32[256,2]{1,0:T(8,128)S(1)} %copy.138), kind=kCustom, calls=%fused_computation.4 | custom fusion | bytes 8192 | tf_op jit(solution)/shard_map/scatter | solution.py:70
  22.5 0.8 copy.139
  23.3 8.4 %all-to-all-start = ((s32[16,8,2]{1,2,0:T(2,128)}), s32[16,8,2]{1,2,0:T(2,128)S(1)}, u32[]{:S(2)}, u32[]{:S(2)}) async-start(s32[16,8,2]{1,2,0:T(2,128)} %copy.139), calls=%async_computation | async-start | bytes 32768 | tf_op jit(solution)/shard_map/all_to_all | solution.py:72
  31.7 3.6 copy.160
  35.3 3.0 copy.140
  39.2 4.5 %gather_fusion = bf16[128,64,128]{2,1,0:T(8,128)(2,1)} fusion(bf16[16,64,16,128]{3,1,2,0:T(8,128)(2,1)} %copy.140, s32[128]{0:T(128)S(1)} %reshape.182), kind=kCustom, calls=%fused_computation | custom fusion | bytes 4195328 | tf_op jit(solution)/shard_map/gather | solution.py:73
  43.6 6.2 %all-to-all-start.1 = ((bf16[16,8,64,128]{3,2,1,0:T(8,128)(2,1)}), bf16[16,8,64,128]{3,2,1,0:T(8,128)(2,1)S(1)}, u32[]{:S(2)}, u32[]{:S(2)}) async-start(bf16[16,8,64,128]{3,2,1,0:T(8,128)(2,1)} %bitcast.114), calls=%async_computation.1 | async-start | bytes 4194304 | tf_op jit(solution)/shard_map/all_to_all | solution.py:75
  49.9 3.6 copy.163
  53.4 3.0 copy.146
  56.5 4.6 %gather_fusion.2 = bf16[128,64,128]{2,1,0:T(8,128)(2,1)} fusion(bf16[16,64,16,128]{3,1,2,0:T(8,128)(2,1)} %copy.146, s32[128]{0:T(128)S(1)} %reshape.182), kind=kCustom, calls=%fused_computation.2 | custom fusion | bytes 4195328 | tf_op jit(solution)/shard_map/gather | solution.py:74
  61.1 37.8 %all-to-all-done.1 = bf16[16,8,64,128]{3,2,1,0:T(8,128)(2,1)S(1)} async-done(((bf16[16,8,64,128]{3,2,1,0:T(8,128)(2,1)}), bf16[16,8,64,128]{3,2,1,0:T(8,128)(2,1)S(1)}, u32[]{:S(2)}, u32[]{:S(2)}) %all-to-all-start.1) | async-done | bytes 2097184 | tf_op jit(solution)/shard_map/all_to_all | solution.py:75
  98.9 10.5 %all-to-all-start.2 = ((bf16[16,8,64,128]{3,2,1,0:T(8,128)(2,1)}), bf16[16,8,64,128]{3,2,1,0:T(8,128)(2,1)}, u32[]{:S(2)}, u32[]{:S(2)}) async-start(bf16[16,8,64,128]{3,2,1,0:T(8,128)(2,1)} %bitcast.113), calls=%async_computation.2 | async-start | bytes 4194304 | tf_op jit(solution)/shard_map/all_to_all | solution.py:76
  110.0 1.5 copy.162
  111.5 1.2 copy.164
  113.0 2.1 fusion.12
  115.1 2.3 copy.125
  117.3 4.2 %multiply_reduce_fusion = (f32[16,256]{1,0:T(8,128)S(1)}, f32[16,256,256]{1,2,0:T(8,128)}) fusion(bf16[256,16,128]{0,2,1:T(8,128)(2,1)} %bitcast.121, bf16[256,2048]{1,0:T(8,128)(2,1)} %param.9), kind=kOutput, calls=%fused_computation.13 | convolution fusion | flops 270528512 | bytes 6307840 | tf_op jit(solution)/shard_map/qhd,nhd->hqn/dot_general | solution.py:38
  121.7 2.9 fusion.2
  124.6 27.3 %all-gather.6.cloned.1.call-done = bf16[256,2048]{1,0:T(8,128)(2,1)} async-done(((bf16[16,2048]{1,0:T(8,128)(2,1)}), bf16[256,2048]{1,0:T(8,128)(2,1)}) %all-gather.6.cloned.1.call-update) | async-done | bytes 1048592 | tf_op jit(solution)/shard_map/all_gather | solution.py:34
  152.0 2.3 copy.128
  154.2 5.2 %fusion.13 = f32[16,256,128]{2,1,0:T(8,128)} fusion(bf16[256,16,128]{0,2,1:T(8,128)(2,1)} %bitcast.115, f32[16,256,256]{1,2,0:T(8,128)} %get-tuple-element.15, f32[16,256]{1,0:T(8,128)S(1)} %get-tuple-element.14, f32[16,256]{1,0:T(8,128)S(1)} %exponential_multiply_fusion), kind=kOutput, calls=%fused_computation.29 | convolution fusion | flops 272105472 | bytes 7372800 | tf_op jit(solution)/shard_map/hqn,nhd->hqd/dot_general | solution.py:45
  159.4 3.4 gather_fusion.1
  162.8 7.2 %bitcast_reduce_fusion = (f32[4,16,64]{2,1,0:T(8,128)S(1)}, f32[4,16,4,64,64]{4,3,2,1,0:T(8,128)}) fusion(bf16[4,16,4,64,128]{4,3,2,1,0:T(8,128)(2,1)} %bitcast.108, bf16[4,64,16,128,1]{3,2,1,0,4:T(8,128)(2,1)S(1)} %bitcast_bitcast_fusion), kind=kOutput, calls=%fused_computation.6 | convolution fusion | flops 270528512 | bytes 9453568 | tf_op jit(solution)/shard_map/gqhd,ghpkd->ghqpk/dot_general | solution.py:85
  170.0 6.8 %copy.145 = f32[4,16,64,256]{3,2,1,0:T(8,128)} copy(f32[4,16,64,256]{2,3,1,0:T(8,128)} %bitcast.107) | data formatting | bytes 8388608 | tf_op jit(solution)/shard_map/reshape | solution.py:90
  176.8 5.1 %gather_fusion.3 = bf16[256,64,128]{2,1,0:T(8,128)(2,1)} fusion(bf16[16,8,64,128]{3,2,1,0:T(8,128)(2,1)} %all-to-all-done.2, s32[256]{0:T(256)S(1)} %reshape.188), kind=kCustom, calls=%fused_computation.3 | custom fusion | bytes 8390656 | tf_op jit(solution)/shard_map/gather | solution.py:80
  182.6 5.5 %fusion.1 = f32[4,16,64]{2,1,0:T(8,128)S(1)} fusion(f32[4,16,4,64,64]{4,3,2,1,0:T(8,128)} %get-tuple-element.13, f32[4,16,64]{2,1,0:T(8,128)S(1)} %fusion.42), kind=kLoop, calls=%fused_computation.8 | loop fusion | flops 2093056 | bytes 4227072 | tf_op jit(solution)/shard_map/reduce_sum | solution.py:109
  188.5 1.2 fusion.6
  190.4 2.0 fusion.8
  193.1 197.3 %all-gather.8.cloned.1.call-done = bf16[2048,4096]{1,0:T(8,128)(2,1)} async-done(((bf16[2048,256]{1,0:T(8,128)(2,1)}), bf16[2048,4096]{1,0:T(8,128)(2,1)}) %all-gather.8.cloned.1.call-update) | async-done | bytes 16777232 | tf_op jit(solution)/shard_map/all_gather | solution.py:128
  390.4 11.5 %convolution_convert_fusion = bf16[256,4096]{1,0:T(8,128)(2,1)} fusion(bf16[2048,4096]{1,0:T(8,128)(2,1)} %all-gather.8.cloned.1.call-done, bf16[32,8,16,128]{3,2,1,0:T(8,128)(2,1)S(1)} %bitcast.127), kind=kOutput, calls=%fused_computation.9 | convolution fusion | flops 4296015872 | bytes 19922944 | tf_op jit(solution)/shard_map/dot_general | solution.py:126
  401.9 8.0 %reduce-scatter.2.cloned.1.call-done = bf16[256,2048]{1,0:T(8,128)(2,1)} async-done(((bf16[256,4096]{1,0:T(8,128)(2,1)}), bf16[256,2048]{1,0:T(8,128)(2,1)}) %reduce-scatter.2.cloned.1.call-update) | async-done | bytes 1048592 | tf_op jit(solution)/shard_map/reduce_scatter | solution.py:131
  (55 shorter events, 7.7 us)
Async XLA Ops:
  6.5 108.5 %all-gather.4.cloned.1.call-start = ((), (), s32[]{:S(2)}) async-start(), calls=%async_computation.4 | async-start | bytes 1114112 | tf_op jit(solution)/shard_map/all_gather | solution.py:31
  7.3 144.7 %all-gather.6.cloned.1.call-start = ((), (), s32[]{:S(2)}) async-start(), calls=%async_computation.5 | async-start | bytes 1114112 | tf_op jit(solution)/shard_map/all_gather | solution.py:34
  8.0 382.4 %all-gather.8.cloned.1.call-start = ((), (), s32[]{:S(2)}) async-start(), calls=%async_computation.6 | async-start | bytes 17825792 | tf_op jit(solution)/shard_map/all_gather | solution.py:128
  23.3 15.7 %all-to-all-start = ((s32[16,8,2]{1,2,0:T(2,128)}), s32[16,8,2]{1,2,0:T(2,128)S(1)}, u32[]{:S(2)}, u32[]{:S(2)}) async-start(s32[16,8,2]{1,2,0:T(2,128)} %copy.139), calls=%async_computation | async-start | bytes 32768 | tf_op jit(solution)/shard_map/all_to_all | solution.py:72
  43.6 55.3 %all-to-all-start.1 = ((bf16[16,8,64,128]{3,2,1,0:T(8,128)(2,1)}), bf16[16,8,64,128]{3,2,1,0:T(8,128)(2,1)S(1)}, u32[]{:S(2)}, u32[]{:S(2)}) async-start(bf16[16,8,64,128]{3,2,1,0:T(8,128)(2,1)} %bitcast.114), calls=%async_computation.1 | async-start | bytes 4194304 | tf_op jit(solution)/shard_map/all_to_all | solution.py:75
  56.5 53.3 %copy-start.2 = (bf16[256,2048]{1,0:T(8,128)(2,1)S(1)}, bf16[256,2048]{1,0:T(8,128)(2,1)}, u32[]{:S(2)}) copy-start(bf16[256,2048]{1,0:T(8,128)(2,1)} %param.9) | copy-start | bytes 3145732
  98.9 77.9 %all-to-all-start.2 = ((bf16[16,8,64,128]{3,2,1,0:T(8,128)(2,1)}), bf16[16,8,64,128]{3,2,1,0:T(8,128)(2,1)}, u32[]{:S(2)}, u32[]{:S(2)}) async-start(bf16[16,8,64,128]{3,2,1,0:T(8,128)(2,1)} %bitcast.113), calls=%async_computation.2 | async-start | bytes 4194304 | tf_op jit(solution)/shard_map/all_to_all | solution.py:76
  109.4 300.5 %reduce-scatter.2.cloned.1.call-start = ((), (), s32[]{:S(2)}) async-start(), calls=%async_computation.7 | async-start | bytes 3145728 | tf_op jit(solution)/shard_map/reduce_scatter | solution.py:131
  109.7 1.8 copy-start.5
  176.8 5.1 %copy-start.4 = (f32[4,16,64,64]{2,3,1,0:T(8,128)S(1)}, f32[4,16,64,64]{2,3,1,0:T(8,128)}, u32[]{:S(2)}) copy-start(f32[4,16,64,64]{2,3,1,0:T(8,128)} %get-tuple-element.11) | copy-start | bytes 3145732
  182.6 5.5 %copy-start = (f32[4,16,64,256]{3,2,1,0:T(8,128)S(1)}, f32[4,16,64,256]{3,2,1,0:T(8,128)}, u32[]{:S(2)}) copy-start(f32[4,16,64,256]{3,2,1,0:T(8,128)} %copy.145) | copy-start | bytes 12582916
  182.6 5.9 %copy-start.1 = (bf16[256,64,128]{2,1,0:T(8,128)(2,1)S(1)}, bf16[256,64,128]{2,1,0:T(8,128)(2,1)}, u32[]{:S(2)}) copy-start(bf16[256,64,128]{2,1,0:T(8,128)(2,1)} %gather_fusion.3) | copy-start | bytes 12582916
  188.5 1.6 copy-start.3
  188.5 1.9 copy-start.6
Sparse Core Ops, SparseCore 0:
  10.1 65.8 all-gather.3
  78.8 73.1 all-gather.5
  154.7 235.6 all-gather.7
  402.1 7.7 reduce-scatter.1
where the time goes:
time: 417 us; the launch traced here: 416 us
  waiting for transfers between devices  273 us (65%)
  local copies, waits for them, and re-layouts  61.3 us (15%)
  matrix products  33.5 us (8%)
  starting transfers between devices  25.2 us (6%)
  between operations  13.4 us (3%)
  other arithmetic  9.83 us (2%)
    all_gather x1, waiting for transfers between devices, local(): lax.all_gather(out_weight, 'ctx', axis=1, tiled=True)  197 us
    all_to_all x1, waiting for transfers between devices, local(): lax.all_to_all(sent_keys, 'ctx', split_axis=0, concat_axis=0, tiled=True)  37.8 us
    all_gather x1, waiting for transfers between devices, local(): lax.all_gather(land_values, 'ctx', axis=0, tiled=True)  27.3 us
    scatter x2, local copies, waits for them, and re-layouts, local(): jnp.zeros((devices, distinct_most, 2), jnp.int32).at[owners_flat, slot_ids]  12.4 us
    unnamed x20, local copies, waits for them, and re-layouts  12 us
    dot_general x1, matrix products, local(): jnp.dot(attended, lax.all_gather(out_weight, 'ctx', axis=1, tiled=True),...  11.5 us
    all_to_all x1, starting transfers between devices, local(): lax.all_to_all(sent_values, 'ctx', split_axis=0, concat_axis=0, tiled=True)  10.5 us
    all_to_all x1, starting transfers between devices, local(): lax.all_to_all(wanted, 'ctx', split_axis=0, concat_axis=0, tiled=True)  8.35 us
  transfers between devices with their start and end apart: 7, of which 5 were waited for; matrix products, arithmetic and copies ran while one was open for 22% of the time, Pallas kernels for 0%

commit v1 on v0

--- a/solution.py
+++ b/solution.py
@@ -125,7 +125,7 @@
     attended = jnp.transpose(attended, (0, 2, 1, 3)).reshape(query_rows, row_width)
     partial_out = jnp.dot(
         attended,
-        lax.all_gather(out_weight, "ctx", axis=1, tiled=True),
+        jnp.concatenate(lax.all_gather(out_weight, "ctx"), 1),
         preferred_element_type=jnp.float32,
     )
     summed = lax.psum_scatter(

time: 417 us -> 402 us (0.964)
  waiting for transfers between devices: 273 us -> 230 us
  local copies, waits for them, and re-layouts: 61.3 us -> 83 us
  matrix products: 33.5 us -> 40.1 us
    all_gather x1, waiting for transfers between devices: 197 us -> 154 us  [local(): lax.all_gather(out_weight, 'ctx')]
    reshape x0 -> x1, local copies, waits for them, and re-layouts: none -> 21.7 us  [local(): jnp.concatenate(lax.all_gather(out_weight, 'ctx'), 1)]
    dot_general x1, matrix products: 11.5 us -> 18 us  [local(): jnp.dot(attended, jnp.concatenate(lax.all_gather(out_weight, 'ctx'), 1),...]
  transfers between devices with their start and end apart: 7 -> 7, of which waited for: 5 -> 5; matrix products, arithmetic and copies ran while one was open for 22% -> 23% of each run, Pallas kernels for 0% -> 0%
where the time goes in v1:
time: 402 us; the launch traced here: 401 us
  waiting for transfers between devices  230 us (57%)
  local copies, waits for them, and re-layouts  83 us (21%)
  matrix products  40.1 us (10%)
  starting transfers between devices  25.2 us (6%)
  between operations  13.4 us (3%)
  other arithmetic  9.87 us (2%)
    all_gather x1, waiting for transfers between devices, local(): lax.all_gather(out_weight, 'ctx')  154 us
    all_to_all x1, waiting for transfers between devices, local(): lax.all_to_all(sent_keys, 'ctx', split_axis=0, concat_axis=0, tiled=True)  37.8 us
    all_gather x1, waiting for transfers between devices, local(): lax.all_gather(land_values, 'ctx', axis=0, tiled=True)  27.3 us
    reshape x1, local copies, waits for them, and re-layouts, local(): jnp.concatenate(lax.all_gather(out_weight, 'ctx'), 1)  21.7 us
    dot_general x1, matrix products, local(): jnp.dot(attended, jnp.concatenate(lax.all_gather(out_weight, 'ctx'), 1),...  18 us
    scatter x2, local copies, waits for them, and re-layouts, local(): jnp.zeros((devices, distinct_most, 2), jnp.int32).at[owners_flat, slot_ids]  12.4 us
    unnamed x20, local copies, waits for them, and re-layouts  11.9 us
    all_to_all x1, starting transfers between devices, local(): lax.all_to_all(sent_values, 'ctx', split_axis=0, concat_axis=0, tiled=True)  10.5 us
  transfers between devices with their start and end apart: 7, of which 5 were waited for; matrix products, arithmetic and copies ran while one was open for 23% of the time, Pallas kernels for 0%

profile of v1, /device:TPU:0, one launch (start us, length us, event | category | flops | bytes accessed | tf_op | source)
XLA Modules:
  0.0 401.2 jit_solution(17739332547592085745)
XLA Ops:
  8.7 0.8 copy.136
  10.9 11.6 %scatter_fusion = s32[16,8,2]{2,1,0:T(8,128)S(1)} fusion(s32[16,8,2]{2,1,0:T(8,128)S(1)} %broadcast_in_dim.38, s32[256]{0:T(256)S(1)} %bitcast.113, s32[256,2]{1,0:T(8,128)S(1)} %copy.141), kind=kCustom, calls=%fused_computation.4 | custom fusion | bytes 8192 | tf_op jit(solution)/shard_map/scatter | solution.py:70
  23.3 8.4 %all-to-all-start = ((s32[16,8,2]{1,2,0:T(2,128)}), s32[16,8,2]{1,2,0:T(2,128)S(1)}, u32[]{:S(2)}, u32[]{:S(2)}) async-start(s32[16,8,2]{1,2,0:T(2,128)} %copy.142), calls=%async_computation | async-start | bytes 32768 | tf_op jit(solution)/shard_map/all_to_all | solution.py:72
  31.7 3.6 copy.164
  35.3 3.0 copy.143
  39.2 4.5 %gather_fusion = bf16[128,64,128]{2,1,0:T(8,128)(2,1)} fusion(bf16[16,64,16,128]{3,1,2,0:T(8,128)(2,1)} %copy.143, s32[128]{0:T(128)S(1)} %reshape.190), kind=kCustom, calls=%fused_computation | custom fusion | bytes 4195328 | tf_op jit(solution)/shard_map/gather | solution.py:73
  43.6 6.2 %all-to-all-start.1 = ((bf16[16,8,64,128]{3,2,1,0:T(8,128)(2,1)}), bf16[16,8,64,128]{3,2,1,0:T(8,128)(2,1)S(1)}, u32[]{:S(2)}, u32[]{:S(2)}) async-start(bf16[16,8,64,128]{3,2,1,0:T(8,128)(2,1)} %bitcast.120), calls=%async_computation.1 | async-start | bytes 4194304 | tf_op jit(solution)/shard_map/all_to_all | solution.py:75
  49.9 3.6 copy.167
  53.4 3.0 copy.149
  56.5 4.6 %gather_fusion.2 = bf16[128,64,128]{2,1,0:T(8,128)(2,1)} fusion(bf16[16,64,16,128]{3,1,2,0:T(8,128)(2,1)} %copy.149, s32[128]{0:T(128)S(1)} %reshape.190), kind=kCustom, calls=%fused_computation.2 | custom fusion | bytes 4195328 | tf_op jit(solution)/shard_map/gather | solution.py:74
  61.1 37.8 %all-to-all-done.1 = bf16[16,8,64,128]{3,2,1,0:T(8,128)(2,1)S(1)} async-done(((bf16[16,8,64,128]{3,2,1,0:T(8,128)(2,1)}), bf16[16,8,64,128]{3,2,1,0:T(8,128)(2,1)S(1)}, u32[]{:S(2)}, u32[]{:S(2)}) %all-to-all-start.1) | async-done | bytes 2097184 | tf_op jit(solution)/shard_map/all_to_all | solution.py:75
  98.9 10.5 %all-to-all-start.2 = ((bf16[16,8,64,128]{3,2,1,0:T(8,128)(2,1)}), bf16[16,8,64,128]{3,2,1,0:T(8,128)(2,1)}, u32[]{:S(2)}, u32[]{:S(2)}) async-start(bf16[16,8,64,128]{3,2,1,0:T(8,128)(2,1)} %bitcast.119), calls=%async_computation.2 | async-start | bytes 4194304 | tf_op jit(solution)/shard_map/all_to_all | solution.py:76
  110.0 1.5 copy.166
  111.5 1.2 copy.168
  113.0 2.1 fusion.12
  115.1 2.3 copy.128
  117.3 4.2 %multiply_reduce_fusion = (f32[16,256]{1,0:T(8,128)S(1)}, f32[16,256,256]{1,2,0:T(8,128)}) fusion(bf16[256,16,128]{0,2,1:T(8,128)(2,1)} %bitcast.127, bf16[256,2048]{1,0:T(8,128)(2,1)} %param.9), kind=kOutput, calls=%fused_computation.13 | convolution fusion | flops 270528512 | bytes 6307840 | tf_op jit(solution)/shard_map/qhd,nhd->hqn/dot_general | solution.py:38
  121.7 2.9 fusion.2
  124.6 27.3 %all-gather.7.cloned.1.call-done = bf16[256,2048]{1,0:T(8,128)(2,1)} async-done(((bf16[16,2048]{1,0:T(8,128)(2,1)}), bf16[256,2048]{1,0:T(8,128)(2,1)}) %all-gather.7.cloned.1.call-update) | async-done | bytes 1048592 | tf_op jit(solution)/shard_map/all_gather | solution.py:34
  152.0 2.3 copy.131
  154.2 5.2 %fusion.13 = f32[16,256,128]{2,1,0:T(8,128)} fusion(bf16[256,16,128]{0,2,1:T(8,128)(2,1)} %bitcast.121, f32[16,256,256]{1,2,0:T(8,128)} %get-tuple-element.15, f32[16,256]{1,0:T(8,128)S(1)} %get-tuple-element.14, f32[16,256]{1,0:T(8,128)S(1)} %exponential_multiply_fusion), kind=kOutput, calls=%fused_computation.29 | convolution fusion | flops 272105472 | bytes 7372800 | tf_op jit(solution)/shard_map/hqn,nhd->hqd/dot_general | solution.py:45
  159.4 3.4 gather_fusion.1
  162.8 7.2 %bitcast_reduce_fusion = (f32[4,16,64]{2,1,0:T(8,128)S(1)}, f32[4,16,4,64,64]{4,3,2,1,0:T(8,128)}) fusion(bf16[4,16,4,64,128]{4,3,2,1,0:T(8,128)(2,1)} %bitcast.112, bf16[4,64,16,128,1]{3,2,1,0,4:T(8,128)(2,1)S(1)} %bitcast_bitcast_fusion), kind=kOutput, calls=%fused_computation.6 | convolution fusion | flops 270528512 | bytes 9453568 | tf_op jit(solution)/shard_map/gqhd,ghpkd->ghqpk/dot_general | solution.py:85
  170.0 6.8 %copy.148 = f32[4,16,64,256]{3,2,1,0:T(8,128)} copy(f32[4,16,64,256]{2,3,1,0:T(8,128)} %bitcast.111) | data formatting | bytes 8388608 | tf_op jit(solution)/shard_map/reshape | solution.py:90
  176.9 5.1 %gather_fusion.3 = bf16[256,64,128]{2,1,0:T(8,128)(2,1)} fusion(bf16[16,8,64,128]{3,2,1,0:T(8,128)(2,1)} %all-to-all-done.2, s32[256]{0:T(256)S(1)} %reshape.196), kind=kCustom, calls=%fused_computation.3 | custom fusion | bytes 8390656 | tf_op jit(solution)/shard_map/gather | solution.py:80
  182.7 5.5 %fusion.1 = f32[4,16,64]{2,1,0:T(8,128)S(1)} fusion(f32[4,16,4,64,64]{4,3,2,1,0:T(8,128)} %get-tuple-element.13, f32[4,16,64]{2,1,0:T(8,128)S(1)} %fusion.42), kind=kLoop, calls=%fused_computation.8 | loop fusion | flops 2093056 | bytes 4227072 | tf_op jit(solution)/shard_map/reduce_sum | solution.py:109
  188.5 1.2 fusion.6
  190.4 2.0 fusion.8
  193.1 153.7 %all-gather.9.cloned.1.call-done = bf16[32768,256]{1,0:T(8,128)(2,1)} async-done(((bf16[2048,256]{1,0:T(8,128)(2,1)}), bf16[32768,256]{1,0:T(8,128)(2,1)}) %all-gather.9.cloned.1.call-update) | async-done | bytes 16777232 | tf_op jit(solution)/shard_map/all_gather | solution.py:128
  346.9 21.7 %copy.155 = bf16[2048,16,256]{0,2,1:T(8,128)(2,1)} copy(bf16[2048,16,256]{2,0,1:T(8,128)(2,1)} %bitcast.114) | data formatting | bytes 33554432 | tf_op jit(solution)/shard_map/reshape | solution.py:128
  368.6 18.0 %convolution_convert_fusion = bf16[256,4096]{1,0:T(8,128)(2,1)} fusion(bf16[2048,4096]{0,1:T(8,128)(2,1)} %bitcast.115, bf16[32,8,16,128]{3,2,1,0:T(8,128)(2,1)S(1)} %bitcast.133), kind=kOutput, calls=%fused_computation.9 | convolution fusion | flops 4296015872 | bytes 19922944 | tf_op jit(solution)/shard_map/dot_general | solution.py:126
  386.7 8.0 %reduce-scatter.2.cloned.1.call-done = bf16[256,2048]{1,0:T(8,128)(2,1)} async-done(((bf16[256,4096]{1,0:T(8,128)(2,1)}), bf16[256,2048]{1,0:T(8,128)(2,1)}) %reduce-scatter.2.cloned.1.call-update) | async-done | bytes 1048592 | tf_op jit(solution)/shard_map/reduce_scatter | solution.py:131
  (56 shorter events, 8.4 us)
Async XLA Ops:
  6.5 108.5 %all-gather.5.cloned.1.call-start = ((), (), s32[]{:S(2)}) async-start(), calls=%async_computation.4 | async-start | bytes 1114112 | tf_op jit(solution)/shard_map/all_gather | solution.py:31
  7.3 144.7 %all-gather.7.cloned.1.call-start = ((), (), s32[]{:S(2)}) async-start(), calls=%async_computation.5 | async-start | bytes 1114112 | tf_op jit(solution)/shard_map/all_gather | solution.py:34
  8.0 338.9 %all-gather.9.cloned.1.call-start = ((), (), s32[]{:S(2)}) async-start(), calls=%async_computation.7 | async-start | bytes 17825792 | tf_op jit(solution)/shard_map/all_gather | solution.py:128
  23.3 15.7 %all-to-all-start = ((s32[16,8,2]{1,2,0:T(2,128)}), s32[16,8,2]{1,2,0:T(2,128)S(1)}, u32[]{:S(2)}, u32[]{:S(2)}) async-start(s32[16,8,2]{1,2,0:T(2,128)} %copy.142), calls=%async_computation | async-start | bytes 32768 | tf_op jit(solution)/shard_map/all_to_all | solution.py:72
  43.6 55.3 %all-to-all-start.1 = ((bf16[16,8,64,128]{3,2,1,0:T(8,128)(2,1)}), bf16[16,8,64,128]{3,2,1,0:T(8,128)(2,1)S(1)}, u32[]{:S(2)}, u32[]{:S(2)}) async-start(bf16[16,8,64,128]{3,2,1,0:T(8,128)(2,1)} %bitcast.120), calls=%async_computation.1 | async-start | bytes 4194304 | tf_op jit(solution)/shard_map/all_to_all | solution.py:75
  56.5 53.3 %copy-start.2 = (bf16[256,2048]{1,0:T(8,128)(2,1)S(1)}, bf16[256,2048]{1,0:T(8,128)(2,1)}, u32[]{:S(2)}) copy-start(bf16[256,2048]{1,0:T(8,128)(2,1)} %param.9) | copy-start | bytes 3145732
  98.9 78.0 %all-to-all-start.2 = ((bf16[16,8,64,128]{3,2,1,0:T(8,128)(2,1)}), bf16[16,8,64,128]{3,2,1,0:T(8,128)(2,1)}, u32[]{:S(2)}, u32[]{:S(2)}) async-start(bf16[16,8,64,128]{3,2,1,0:T(8,128)(2,1)} %bitcast.119), calls=%async_computation.2 | async-start | bytes 4194304 | tf_op jit(solution)/shard_map/all_to_all | solution.py:76
  109.4 285.2 %reduce-scatter.2.cloned.1.call-start = ((), (), s32[]{:S(2)}) async-start(), calls=%async_computation.6 | async-start | bytes 3145728 | tf_op jit(solution)/shard_map/reduce_scatter | solution.py:131
  109.7 1.8 copy-start.5
  176.9 5.1 %copy-start.4 = (f32[4,16,64,64]{2,3,1,0:T(8,128)S(1)}, f32[4,16,64,64]{2,3,1,0:T(8,128)}, u32[]{:S(2)}) copy-start(f32[4,16,64,64]{2,3,1,0:T(8,128)} %get-tuple-element.11) | copy-start | bytes 3145732
  182.6 5.6 %copy-start = (f32[4,16,64,256]{3,2,1,0:T(8,128)S(1)}, f32[4,16,64,256]{3,2,1,0:T(8,128)}, u32[]{:S(2)}) copy-start(f32[4,16,64,256]{3,2,1,0:T(8,128)} %copy.148) | copy-start | bytes 12582916
  182.7 5.9 %copy-start.1 = (bf16[256,64,128]{2,1,0:T(8,128)(2,1)S(1)}, bf16[256,64,128]{2,1,0:T(8,128)(2,1)}, u32[]{:S(2)}) copy-start(bf16[256,64,128]{2,1,0:T(8,128)(2,1)} %gather_fusion.3) | copy-start | bytes 12582916
  188.5 1.6 copy-start.3
  188.5 1.9 copy-start.6
Sparse Core Ops, SparseCore 0:
  10.1 65.8 all-gather.4
  78.8 73.1 all-gather.6
  154.7 192.0 all-gather.8
  386.8 7.8 reduce-scatter.1
